TPU v7x, 256 devices: a whole 4x4x8 slice. The times are simulated.
256 devices in a mesh: grp: 8 (over x, core), dev: 32 (over z, y).
Axes of the slice: x: 4, y: 4, z: 8, core: 2. Of those that a mesh axis runs over, the one named last changes fastest.
Arguments:
- points: bfloat16 [524288, 1024], P(('grp', 'dev')), may hold values from -6 to 6
- blocks: int32 [524288, 1], P(('grp', 'dev')), may hold values from 0 to 255; in each aligned block of 2048 rows (0 to 2047, 2048 to 4095, ...) at most 16 rows name the same one
- finals: int32 [524288], P(('grp', 'dev')), may hold values from 0 to 255
- centroids: bfloat16 [65536, 1024], P('dev'), may hold values from -6 to 6
Outputs:
- distances: bfloat16 [524288, 256], P(('grp', 'dev'))
- refreshed_centroids: float32 [65536, 1024], P('dev', 'grp')
Inputs may be any that keep to these rules, and one draw needn't show every extreme that they name: `blocks`: among the 2048 rows of one device no block is named by more than 16 rows, and some block by exactly 16. Block b is held by index b // 8 of dev. The point's centroid is row 256 * blocks + finals of centroids.
All inputs are finite; a program needn't handle non-finite values.
Results may differ from a plain program's by a relative error of at most 0.008.
Values may be sent and summed in bfloat16 or wider, within the bound.
No kernel may reach another device: no remote copies, remote signals or barrier semaphores. Data moves between devices by JAX's collectives and lax.ppermute only.
A program may use at most 128 MiB of HBM per device.

v0:
```python
import jax
import jax.numpy as jnp
from jax import lax
from jax.sharding import PartitionSpec as P

BS = 256


def block_work(received_points, wanted, centroid_table, width, block_size):
    cent_norm = jnp.sum(jnp.square(centroid_table.astype(jnp.float32)), axis=-1)
    row_norm = jnp.sum(jnp.square(received_points.astype(jnp.float32)), axis=-1)
    cross_products = jnp.einsum(
        "nzy,nvy->nzv", received_points, centroid_table, preferred_element_type=jnp.float32
    )
    dists = ((row_norm[:, :, None] - 2.0 * cross_products + cent_norm[:, None, :]) / width).astype(
        jnp.bfloat16
    )
    onehot_assign = wanted[:, :, None] == jnp.arange(block_size, dtype=jnp.int32)[None, None, :]
    sums = jnp.einsum(
        "xnt,xni->xti",
        onehot_assign.astype(jnp.bfloat16),
        received_points,
        preferred_element_type=jnp.float32,
    )
    counts = jnp.sum(onehot_assign.astype(jnp.float32), axis=1)
    return (dists, sums, counts)


def shards(points, blocks, finals, centroids):
    shard_counts = lax.axis_size("dev")
    count_grp = lax.axis_size("grp")
    npoints, width = points.shape
    block_size = BS
    owned = centroids.shape[0] // block_size
    nblocks = owned * shard_counts
    depth = 2 * npoints // nblocks
    block_ids = blocks[:, 0]
    labels = jnp.arange(nblocks, dtype=jnp.int32)
    member = block_ids[:, None] == labels[None, :]
    lower = (jnp.arange(npoints)[:, None] > jnp.arange(npoints)[None, :]).astype(jnp.bfloat16)
    before = jnp.dot(lower, member.astype(jnp.bfloat16), preferred_element_type=jnp.float32)
    ranks = jnp.sum(jnp.where(member, before, 0.0), axis=1).astype(jnp.int32)
    slots = block_ids * depth + ranks
    outgoing = jnp.zeros((nblocks * depth, width), jnp.bfloat16).at[slots].set(points)
    targets = jnp.full((nblocks * depth,), -1, jnp.int32).at[slots].set(finals)
    outgoing = outgoing.reshape(nblocks, depth, width)
    targets = targets.reshape(nblocks, depth)
    received_points, wanted = (
        lax.all_to_all(outgoing, "dev", split_axis=0, concat_axis=1, tiled=True),
        lax.all_to_all(targets, "dev", split_axis=0, concat_axis=1, tiled=True),
    )
    centroid_table = centroids.reshape(owned, block_size, width)
    dists, sums, counts = block_work(received_points, wanted, centroid_table, width, block_size)
    sums = sums.reshape(owned * block_size, width)
    counts = counts.reshape(owned * block_size)
    returned = lax.all_to_all(dists, "dev", split_axis=1, concat_axis=0, tiled=True)
    distances = returned.reshape(nblocks * depth, block_size)[slots]
    part_sums, part_counts = (
        lax.psum_scatter(sums.astype(jnp.bfloat16), "grp", scatter_dimension=0, tiled=True).astype(
            jnp.float32
        ),
        lax.psum_scatter(
            counts.astype(jnp.bfloat16), "grp", scatter_dimension=0, tiled=True
        ).astype(jnp.float32),
    )
    rows_here = sums.shape[0] // count_grp
    own_rows = lax.dynamic_slice_in_dim(
        centroids, lax.axis_index("grp") * rows_here, rows_here, 0
    ).astype(jnp.float32)
    fresh = (part_sums + own_rows) / (part_counts + 1.0)[:, None]
    refreshed_centroids = lax.all_to_all(
        fresh.astype(jnp.bfloat16), "grp", split_axis=1, concat_axis=0, tiled=True
    ).astype(fresh.dtype)
    return (distances, refreshed_centroids)


def solution(mesh):
    placed = (P(("grp", "dev"), None), P(("grp", "dev"), None), P(("grp", "dev")), P("dev", None))
    return jax.shard_map(
        shards,
        mesh=mesh,
        in_specs=placed,
        out_specs=(P(("grp", "dev"), None), P("dev", "grp")),
        check_vma=False,
    )
```

profile of v0, /device:TPU:1, one launch (start us, length us, event | category | flops | bytes accessed | tf_op | source)
XLA Modules:
  0.0 362.5 jit_solution(12675726830021079699)
XLA Ops:
  7.2 3.2 fusion.7
  10.4 8.2 %scatter_custom_fusion.1 = s32[4096]{0:T(1024)S(1)} fusion(s32[2048]{0:T(1024)S(1)} %bitcast.40, s32[2048]{0:T(1024)} %param.6, s32[]{:T(128)} %constant.9.clone.1), kind=kCustom, calls=%fused_computation.23 | custom fusion | bytes 16896 | tf_op jit(solution)/shard_map/scatter | solution.py:45
  18.8 0.7 reshape.78
  19.5 12.0 %all-to-all-start.2 = ((s32[32,1,128]{2,1,0:T(1,128)}), s32[32,1,128]{2,1,0:T(1,128)S(1)}, u32[]{:S(2)}, u32[]{:S(2)}) async-start(s32[32,1,128]{2,1,0:T(1,128)} %reshape.78), calls=%async_computation.2 | async-start | bytes 32768 | tf_op jit(solution)/shard_map/all_to_all | solution.py:50
  31.5 15.2 %scatter_custom_fusion = bf16[4096,1024]{1,0:T(8,128)(2,1)} fusion(s32[2048]{0:T(1024)S(1)} %bitcast.41, bf16[2048,1024]{1,0:T(8,128)(2,1)} %param.4, bf16[]{:T(256)} %constant.13.clone.1), kind=kCustom, calls=%fused_computation.11 | custom fusion | bytes 8389120 | tf_op jit(solution)/shard_map/scatter | solution.py:44
  46.8 9.3 %all-to-all-start = ((bf16[256,16,1024]{2,1,0:T(8,128)(2,1)}), bf16[256,16,1024]{2,1,0:T(8,128)(2,1)}, u32[]{:S(2)}, u32[]{:S(2)}) async-start(bf16[256,16,1024]{2,1,0:T(8,128)(2,1)} %bitcast.32), calls=%async_computation | async-start | bytes 16777216 | tf_op jit(solution)/shard_map/all_to_all | solution.py:49
  56.3 0.5 broadcast.19
  56.9 0.7 reduce.2
  57.8 189.4 %all-to-all-done = bf16[256,16,1024]{2,1,0:T(8,128)(2,1)} async-done(((bf16[256,16,1024]{2,1,0:T(8,128)(2,1)}), bf16[256,16,1024]{2,1,0:T(8,128)(2,1)}, u32[]{:S(2)}, u32[]{:S(2)}) %all-to-all-start) | async-done | bytes 8388640 | tf_op jit(solution)/shard_map/all_to_all | solution.py:49
  247.2 8.5 %copy.13 = bf16[8,32,16,1024]{3,2,1,0:T(8,128)(2,1)} copy(bf16[8,32,16,1024]{3,2,0,1:T(8,128)(2,1)} %bitcast.5) | data formatting | bytes 16777216 | tf_op jit(solution)/shard_map/all_to_all | solution.py:49
  255.7 7.7 %fusion.5 = bf16[8,256,1024]{2,1,0:T(8,128)(2,1)} fusion(bf16[8,512,1024]{2,1,0:T(8,128)(2,1)} %bitcast.33, s32[8,512]{1,0:T(8,128)S(1)} %eq.34), kind=kOutput, calls=%fused_computation.14 | convolution fusion | flops 2150629376 | bytes 12599296 | tf_op jit(solution)/shard_map/xnt,xni->xti/dot_general | solution.py:19
  263.4 3.1 multiply_reduce_fusion.1
  266.4 5.1 %multiply_reduce_fusion = f32[8,32,16]{2,0,1:T(8,128)S(1)} fusion(bf16[8,32,16,1024]{3,2,0,1:T(8,128)(2,1)} %bitcast.5), kind=kLoop, calls=%fused_computation.3 | loop fusion | flops 12578816 | bytes 8404992 | tf_op jit(solution)/shard_map/reduce_sum | solution.py:11
  271.7 7.5 %multiply_convert_fusion = bf16[8,512,256]{2,1,0:T(8,128)(2,1)S(1)} fusion(bf16[8,512,1024]{2,1,0:T(8,128)(2,1)} %bitcast.34, bf16[8,256,1024]{2,1,0:T(8,128)(2,1)} %bitcast.36, f32[8,256]{1,0:T(8,128)S(1)} %add.38, f32[8,512]{1,0:T(8,128)S(1)} %sub.10), kind=kOutput, calls=%fused_computation.10 | convolution fusion | flops 2152726528 | bytes 14704640 | tf_op jit(solution)/shard_map/nzy,nvy->nzv/dot_general | solution.py:12
  279.2 2.5 copy.14
  281.8 6.2 %all-to-all-start.1 = ((bf16[8,512,256]{2,0,1:T(8,128)(2,1)}), bf16[8,512,256]{2,0,1:T(8,128)(2,1)S(1)}, u32[]{:S(2)}, u32[]{:S(2)}) async-start(bf16[8,512,256]{2,0,1:T(8,128)(2,1)} %copy.14), calls=%async_computation.1 | async-start | bytes 4194304 | tf_op jit(solution)/shard_map/all_to_all | solution.py:56
  288.0 0.6 dynamic-slice
  289.7 14.1 %all-reduce = bf16[2048]{0:T(1024)(128)(2,1)S(1)} all-reduce(bf16[2048]{0:T(1024)(128)(2,1)S(1)} %bitcast.45), channel_id=3, replica_groups=mesh['grp'=8,'dev'=32] {'grp'}, use_global_device_ids=true, to_apply=%region_7.8.clone | all-reduce | flops 2048 | bytes 8192
  303.9 2.2 copy_bitcast_fusion
  306.1 28.7 %all-to-all-done.1 = bf16[8,512,256]{2,0,1:T(8,128)(2,1)S(1)} async-done(((bf16[8,512,256]{2,0,1:T(8,128)(2,1)}), bf16[8,512,256]{2,0,1:T(8,128)(2,1)S(1)}, u32[]{:S(2)}, u32[]{:S(2)}) %all-to-all-start.1) | async-done | bytes 2097184 | tf_op jit(solution)/shard_map/all_to_all | solution.py:56
  334.8 8.5 %all-to-all-start.3 = ((bf16[256,8,128]{2,0,1:T(8,128)(2,1)}), bf16[256,8,128]{2,0,1:T(8,128)(2,1)S(1)}, u32[]{:S(2)}, u32[]{:S(2)}) async-start(bf16[256,8,128]{2,0,1:T(8,128)(2,1)} %copy_bitcast_fusion), calls=%async_computation.4 | async-start | bytes 1048576 | tf_op jit(solution)/shard_map/all_to_all | solution.py:71
  343.4 2.2 copy.15
  345.6 9.1 %gather_fusion = bf16[2048,256]{1,0:T(8,128)(2,1)} fusion(bf16[4096,256]{1,0:T(8,128)(2,1)S(1)} %bitcast.31, s32[2048]{0:T(1024)S(1)} %broadcast_clamp_fusion), kind=kCustom, calls=%fused_computation | custom fusion | bytes 2105344 | tf_op jit(solution)/shard_map/gather | solution.py:57
  354.7 1.0 convert_element_type.81
  (24 shorter events, 1.3 us)
Async XLA Ops:
  7.2 3.2 copy-start.1
  19.5 27.3 %all-to-all-start.2 = ((s32[32,1,128]{2,1,0:T(1,128)}), s32[32,1,128]{2,1,0:T(1,128)S(1)}, u32[]{:S(2)}, u32[]{:S(2)}) async-start(s32[32,1,128]{2,1,0:T(1,128)} %reshape.78), calls=%async_computation.2 | async-start | bytes 32768 | tf_op jit(solution)/shard_map/all_to_all | solution.py:50
  46.8 200.4 %all-to-all-start = ((bf16[256,16,1024]{2,1,0:T(8,128)(2,1)}), bf16[256,16,1024]{2,1,0:T(8,128)(2,1)}, u32[]{:S(2)}, u32[]{:S(2)}) async-start(bf16[256,16,1024]{2,1,0:T(8,128)(2,1)} %bitcast.32), calls=%async_computation | async-start | bytes 16777216 | tf_op jit(solution)/shard_map/all_to_all | solution.py:49
  56.1 247.8 %reduce-scatter.2.cloned.1.call-start = ((), (), s32[]{:S(2)}) async-start(), calls=%async_computation.5 | async-start | bytes 4718592 | tf_op jit(solution)/shard_map/reduce_scatter | solution.py:59
  279.2 8.8 %copy-start.2 = (u32[256]{0:T(256)S(1)}, u32[256]{0:T(256)}, u32[]{:S(2)}) copy-start(u32[256]{0:T(256)} %constant.32) | copy-start | bytes 3076
  281.8 53.1 %all-to-all-start.1 = ((bf16[8,512,256]{2,0,1:T(8,128)(2,1)}), bf16[8,512,256]{2,0,1:T(8,128)(2,1)S(1)}, u32[]{:S(2)}, u32[]{:S(2)}) async-start(bf16[8,512,256]{2,0,1:T(8,128)(2,1)} %copy.14), calls=%async_computation.1 | async-start | bytes 4194304 | tf_op jit(solution)/shard_map/all_to_all | solution.py:56
  334.8 8.5 %copy-start = (bf16[8,512,256]{2,0,1:T(8,128)(2,1)}, bf16[8,512,256]{2,0,1:T(8,128)(2,1)S(1)}, u32[]{:S(2)}) copy-start(bf16[8,512,256]{2,0,1:T(8,128)(2,1)S(1)} %all-to-all-done.1) | copy-start | bytes 6291460
  334.8 19.8 %all-to-all-start.3 = ((bf16[256,8,128]{2,0,1:T(8,128)(2,1)}), bf16[256,8,128]{2,0,1:T(8,128)(2,1)S(1)}, u32[]{:S(2)}, u32[]{:S(2)}) async-start(bf16[256,8,128]{2,0,1:T(8,128)(2,1)} %copy_bitcast_fusion), calls=%async_computation.4 | async-start | bytes 1048576 | tf_op jit(solution)/shard_map/all_to_all | solution.py:71
Sparse Core Ops, SparseCore 0:
  263.5 36.5 reduce-scatter.1
where the time goes:
time: 363 us
  waiting for transfers between devices  218 us (60%)
  local copies, waits for them, and re-layouts  48.1 us (13%)
  starting transfers between devices  36.3 us (10%)
  matrix products  18.4 us (5%)
  between operations  14.9 us (4%)
  blocking collectives  14.1 us (4%)
  other arithmetic  12.7 us (3%)
    all_to_all x1, waiting for transfers between devices, shards(): lax.all_to_all(outgoing, 'dev', split_axis=0, concat_axis=1, tiled=True)  189 us
    all_to_all x1, waiting for transfers between devices, shards(): lax.all_to_all(dists, 'dev', split_axis=1, concat_axis=0, tiled=True)  28.7 us
    scatter x1, local copies, waits for them, and re-layouts, shards(): jnp.zeros((nblocks * depth, width), jnp.bfloat16).at[slots].set(points)  15.2 us
    unnamed x1, blocking collectives  14.1 us
    all_to_all x1, starting transfers between devices, shards(): lax.all_to_all(targets, 'dev', split_axis=0, concat_axis=1, tiled=True)  12 us
    all_to_all x1, starting transfers between devices, shards(): lax.all_to_all(outgoing, 'dev', split_axis=0, concat_axis=1, tiled=True)  9.35 us
    gather x1, local copies, waits for them, and re-layouts, shards(): distances = returned.reshape(nblocks * depth, block_size)[slots]  9.06 us
    all_to_all x1, starting transfers between devices, shards(): lax.all_to_all(fresh.astype(jnp.bfloat16), 'grp', split_axis=1, concat_ax...  8.54 us
  transfers between devices with their start and end apart: 5, of which 2 were waited for; matrix products, arithmetic and copies ran while one was open for 14% of the time, Pallas kernels for 0%

commit v1 on v0

v1 whole, which is shorter than its diff:
```python
import functools

import jax
import jax.numpy as jnp
from jax import lax
from jax.experimental import pallas as pl
from jax.experimental.pallas import tpu as pltpu
from jax.sharding import Mesh
from jax.sharding import PartitionSpec as P

BS = 256
MOST = 16
NX, NC, NZ, NY = 4, 2, 8, 4
NG = NX * NC
NB = NZ * NY * NG
DESTS = NG * NY
SLOTS = NZ * MOST
WIDTHS = (512, 512)
PLANE = ("x", "c", "y")
PER_STEP = 4
F32, BF16 = jnp.float32, jnp.bfloat16


def nt_dot(a, b):
    return lax.dot_general(a, b, (((1,), (1,)), ((), ())), preferred_element_type=F32)


def tn_dot(a, b):
    return lax.dot_general(a, b, (((0,), (0,)), ((), ())), preferred_element_type=F32)


def slots_of(block_row):
    npts = block_row.shape[1]
    piece = 128
    before = (
        lax.broadcasted_iota(jnp.int32, (piece, piece), 0)
        < lax.broadcasted_iota(jnp.int32, (piece, piece), 1)
    ).astype(BF16)
    carry = jnp.zeros((NB, 1), F32)
    ranks = []
    for i in range(npts // piece):
        part = block_row[:, i * piece : (i + 1) * piece]
        member = lax.broadcasted_iota(jnp.int32, (NB, piece), 0) == part
        ones = jnp.where(member, 1.0, 0.0)
        seen = jnp.dot(ones.astype(BF16), before, preferred_element_type=F32) + carry
        ranks.append(jnp.sum(ones * seen, axis=0, keepdims=True))
        carry = carry + jnp.sum(ones, axis=1, keepdims=True)
    rank = jnp.concatenate(ranks, axis=1).astype(jnp.int32)
    zz = block_row // (NY * NG)
    yy = (block_row // NG) % NY
    gg = block_row % NG
    return ((gg * NY + yy) * NZ + zz) * MOST + rank


def first_prep(block_ref, final_ref, points_ref, out_ref, slot_ref, target_ref, slots):
    step = pl.program_id(0)

    @pl.when(step == 0)
    def _():
        found = slots_of(block_ref[...])
        slots[...] = found
        slot_ref[...] = found

    rows = PER_STEP * SLOTS
    npts = points_ref.shape[0]
    at = step * rows + lax.broadcasted_iota(jnp.int32, (rows, npts), 0)
    pick = jnp.where(at == slots[...], 1.0, 0.0).astype(BF16)
    moved = jnp.dot(pick, points_ref[...], preferred_element_type=F32)
    out_ref[...] = moved.astype(BF16).reshape(out_ref.shape)
    marks = jnp.broadcast_to((final_ref[...] + 1).astype(F32).astype(BF16), (8, npts))
    target = nt_dot(marks, pick)[0:1] - 1.0
    target_ref[...] = target.astype(jnp.int32).reshape(target_ref.shape)


def later_prep(slot_ref, points_ref, out_ref):
    step = pl.program_id(0)
    rows = PER_STEP * SLOTS
    npts = points_ref.shape[0]
    at = step * rows + lax.broadcasted_iota(jnp.int32, (rows, npts), 0)
    pick = jnp.where(at == slot_ref[...], 1.0, 0.0).astype(BF16)
    moved = jnp.dot(pick, points_ref[...], preferred_element_type=F32)
    out_ref[...] = moved.astype(BF16).reshape(out_ref.shape)


def prepare(block_row, final_row, points, start, width, slot_row):
    npts = points.shape[0]
    steps = DESTS // PER_STEP
    column = start // width
    whole = pl.BlockSpec((1, npts), lambda i: (0, 0))
    point_spec = pl.BlockSpec((npts, width), lambda i: (0, column))
    out_spec = pl.BlockSpec((PER_STEP, SLOTS, width), lambda i: (i, 0, 0))
    out_shape = jax.ShapeDtypeStruct((DESTS, SLOTS, width), BF16)
    cost = pl.CostEstimate(
        flops=2 * DESTS * SLOTS * npts * width,
        bytes_accessed=2 * width * (npts + DESTS * SLOTS),
        transcendentals=0,
    )
    if slot_row is not None:
        return pl.pallas_call(
            later_prep,
            grid=(steps,),
            in_specs=[whole, point_spec],
            out_specs=out_spec,
            out_shape=out_shape,
            cost_estimate=cost,
        )(slot_row, points)
    return pl.pallas_call(
        first_prep,
        grid=(steps,),
        in_specs=[whole, whole, point_spec],
        out_specs=(
            out_spec,
            whole,
            pl.BlockSpec((1, 1, PER_STEP * SLOTS), lambda i: (i, 0, 0)),
        ),
        out_shape=(
            out_shape,
            jax.ShapeDtypeStruct((1, npts), jnp.int32),
            jax.ShapeDtypeStruct((steps, 1, PER_STEP * SLOTS), jnp.int32),
        ),
        scratch_shapes=[pltpu.VMEM((1, npts), jnp.int32)],
        cost_estimate=cost,
    )(block_row, final_row, points)


def work_kernel(first, last, *refs):
    refs = list(refs)
    rows_ref, cent_ref, target_ref = refs[:3]
    part_ref = None if first else refs[3]
    sums_ref, result_ref = refs[-2:]
    rows = rows_ref[...].reshape(DESTS * MOST, rows_ref.shape[-1])
    table = cent_ref[0]
    onehot = jnp.where(
        lax.broadcasted_iota(jnp.int32, (BS, DESTS * MOST), 0) == target_ref[0], 1.0, 0.0
    ).astype(BF16)
    sums = jnp.dot(onehot, rows, preferred_element_type=F32)
    sums_ref[0, 0:BS] = sums.astype(BF16)
    if first:
        ones = jnp.ones((8, DESTS * MOST), BF16)
        count = nt_dot(ones, onehot)
        high = jnp.floor(count * (1.0 / 16.0))
        low = count - 16.0 * high
        which = lax.broadcasted_iota(jnp.int32, count.shape, 0)
        digits = jnp.where(which == 0, low, jnp.where(which == 1, high, 0.0))
        extra = sums_ref.shape[-1] - BS
        sums_ref[0, BS : BS + 8, 0:BS] = digits.astype(BF16)
        if extra:
            sums_ref[0, BS : BS + 8, BS:] = jnp.zeros((8, extra), BF16)
    cross = nt_dot(rows, table)
    wide = rows.astype(F32)
    row_norm = jnp.sum(wide * wide, axis=1, keepdims=True)
    tall = table.astype(F32)
    cent_norm = jnp.sum(tall * tall, axis=1, keepdims=True)
    cent_norm = jnp.transpose(jnp.broadcast_to(cent_norm, (BS, 128)))[0:1]
    total = row_norm - 2.0 * cross + cent_norm
    if not first:
        total = total + part_ref[0]
    if last:
        result_ref[...] = (total * (1.0 / 1024.0)).astype(BF16).reshape(result_ref.shape)
    else:
        result_ref[0] = total


def block_work(rows, table, target, part, start, last):
    width = rows.shape[-1]
    first = part is None
    taken = DESTS * MOST
    tall = BS + 8 if first else BS
    row_spec = pl.BlockSpec((DESTS, MOST, width), lambda j: (0, j, 0))
    part_spec = pl.BlockSpec((1, taken, BS), lambda j: (j, 0, 0))
    in_specs = [
        row_spec,
        pl.BlockSpec((1, BS, width), lambda j: (j, 0, start // width)),
        pl.BlockSpec((1, 1, taken), lambda j: (j, 0, 0)),
    ]
    operands = [rows, table, target]
    if not first:
        in_specs.append(part_spec)
        operands.append(part)
    if last:
        result_spec = pl.BlockSpec((DESTS, MOST, BS), lambda j: (0, j, 0))
        result_shape = jax.ShapeDtypeStruct((DESTS, SLOTS, BS), BF16)
    else:
        result_spec = part_spec
        result_shape = jax.ShapeDtypeStruct((NZ, taken, BS), F32)
    return pl.pallas_call(
        functools.partial(work_kernel, first, last),
        grid=(NZ,),
        in_specs=in_specs,
        out_specs=(pl.BlockSpec((1, tall, width), lambda j: (j, 0, 0)), result_spec),
        out_shape=(jax.ShapeDtypeStruct((NZ, tall, width), BF16), result_shape),
        cost_estimate=pl.CostEstimate(
            flops=4 * NZ * taken * BS * width,
            bytes_accessed=2 * width * NZ * (taken + 2 * BS) + 8 * NZ * taken * BS,
            transcendentals=0,
        ),
    )(*operands)


def return_kernel(slot_ref, returned_ref, out_ref):
    rows = out_ref.shape[0]
    total = returned_ref.shape[0]
    slot = jnp.broadcast_to(slot_ref[...].astype(F32), (128, rows))
    column = jnp.transpose(slot)[:, 0:1].astype(jnp.int32)
    pick = jnp.where(
        lax.broadcasted_iota(jnp.int32, (rows, total), 1) == column, 1.0, 0.0
    ).astype(BF16)
    got = jnp.dot(pick, returned_ref[...], preferred_element_type=F32)
    out_ref[...] = got.astype(BF16)


def pick_back(slot_row, returned):
    npts = slot_row.shape[1]
    rows = 256
    return pl.pallas_call(
        return_kernel,
        grid=(npts // rows,),
        in_specs=[
            pl.BlockSpec((1, rows), lambda i: (0, i)),
            pl.BlockSpec(returned.shape, lambda i: (0, 0)),
        ],
        out_specs=pl.BlockSpec((rows, BS), lambda i: (i, 0)),
        out_shape=jax.ShapeDtypeStruct((npts, BS), BF16),
        cost_estimate=pl.CostEstimate(
            flops=2 * npts * returned.shape[0] * BS,
            bytes_accessed=2 * BS * (npts + returned.shape[0]),
            transcendentals=0,
        ),
    )(slot_row, returned)


def exchange(values, axes):
    return lax.all_to_all(values, axes, split_axis=0, concat_axis=0, tiled=True)


def shards(points, blocks, finals, centroids):
    npts, width = points.shape
    group = lax.axis_index("x") * NC + lax.axis_index("c")
    own = lax.dynamic_slice_in_dim(centroids, group * BS, BS, 0)
    table = lax.all_gather(own, "z", axis=0, tiled=False)

    block_row = blocks.reshape(1, npts)
    final_row = finals.reshape(1, npts)
    slot_row = None
    arrived, start = [], 0
    for size in WIDTHS:
        if slot_row is None:
            sent, slot_row, target = prepare(block_row, final_row, points, start, size, None)
            arrived.append(exchange(sent, PLANE))
            target = exchange(target.reshape(DESTS, SLOTS), PLANE)
            target = jnp.transpose(target.reshape(DESTS, NZ, MOST), (1, 0, 2))
            target = target.reshape(NZ, 1, DESTS * MOST)
        else:
            sent = prepare(block_row, final_row, points, start, size, slot_row)
            arrived.append(exchange(sent, PLANE))
        start += size

    part, start, shares = None, 0, []
    for i, size in enumerate(WIDTHS):
        sums, part = block_work(arrived[i], table, target, part, start, i == len(WIDTHS) - 1)
        shares.append(lax.psum_scatter(sums, "z", scatter_dimension=0, tiled=True)[0])
        start += size
    returned = exchange(part, PLANE).reshape(DESTS * SLOTS, BS)
    distances = pick_back(slot_row, returned)

    counts = shares[0][BS, :BS].astype(F32) + 16.0 * shares[0][BS + 1, :BS].astype(F32)
    total = jnp.concatenate([s[:BS].astype(F32) for s in shares], axis=1)
    fresh = (total + own.astype(F32)) / (counts + 1.0)[:, None]
    fresh = lax.all_to_all(fresh.astype(BF16), ("x", "c"), split_axis=1, concat_axis=0, tiled=True)
    return distances, fresh.astype(F32)


def solution(mesh):
    split = Mesh(mesh.devices.reshape(NX, NC, NZ, NY), ("x", "c", "z", "y"))
    every = ("x", "c", "z", "y")
    placed = (P(every, None), P(every, None), P(every), P(("z", "y"), None))
    return jax.shard_map(
        shards,
        mesh=split,
        in_specs=placed,
        out_specs=(P(every, None), P(("z", "y"), ("x", "c"))),
        check_vma=False,
    )
```

time: 363 us -> 254 us (0.70)
  waiting for transfers between devices: 218 us -> 81.6 us
  blocking collectives: 14.1 us -> 73.4 us
  Pallas kernels: 0 us -> 57.3 us
  local copies, waits for them, and re-layouts: 48.1 us -> 3.76 us
  matrix products: 18.4 us -> 0 us
  starting transfers between devices: 36.3 us -> 18.8 us
  other arithmetic: 12.7 us -> 3.92 us
    all_to_all x4 -> x3, waiting for transfers between devices: 218 us -> 49.6 us  [the longest x2 49.6 us: exchange(): return lax.all_to_all(values, axes, split_axis=0, concat_axis=0, tiled=True)]
    all_to_all x0 -> x2, blocking collectives: none -> 73.4 us  [exchange(): return lax.all_to_all(values, axes, split_axis=0, concat_axis=0, tiled=True)]
    pallas_call x0 -> x5, Pallas kernels: none -> 57.3 us  [the longest x2 18.2 us: block_work(): pl.pallas_call(functools.partial(work_kernel, first, last), grid=(NZ,), i...]
    reduce_scatter x1 -> x2, waiting for transfers between devices: 0.01 us -> 32 us  [shards(): lax.psum_scatter(sums, 'z', scatter_dimension=0, tiled=True)[0]]
    scatter x2 -> x0, local copies, waits for them, and re-layouts: 23.5 us -> none  [the longest x1 15.2 us: shards(): jnp.zeros((nblocks * depth, width), jnp.bfloat16).at[slots].set(points)]
    dot_general x3 -> x0, matrix products: 18.4 us -> none  [the longest x1 7.67 us: block_work(): jnp.einsum('xnt,xni->xti', onehot_assign.astype(jnp.bfloat16), received_p...]
    all_to_all x4 -> x3, starting transfers between devices: 36.1 us -> 18.7 us  [the longest x2 9.84 us: exchange(): return lax.all_to_all(values, axes, split_axis=0, concat_axis=0, tiled=True)]
    unnamed x1 -> x0, blocking collectives: 14.1 us -> none
  transfers between devices with their start and end apart: 5 -> 6, of which waited for: 2 -> 2; matrix products, arithmetic and copies ran while one was open for 14% -> 2% of each run, Pallas kernels for 0% -> 19%
where the time goes in v1:
time: 254 us; the launch traced here: 253 us
  waiting for transfers between devices  81.6 us (32%)
  blocking collectives  73.4 us (29%)
  Pallas kernels  57.3 us (23%)
  starting transfers between devices  18.8 us (7%)
  between operations  13.8 us (5%)
  other arithmetic  3.92 us (2%)
  local copies, waits for them, and re-layouts  3.76 us (1%)
    all_to_all x2, blocking collectives, exchange(): return lax.all_to_all(values, axes, split_axis=0, concat_axis=0, tiled=True)  73.4 us
    all_to_all x2, waiting for transfers between devices, exchange(): return lax.all_to_all(values, axes, split_axis=0, concat_axis=0, tiled=True)  49.6 us
    reduce_scatter x2, waiting for transfers between devices, shards(): lax.psum_scatter(sums, 'z', scatter_dimension=0, tiled=True)[0]  32 us
    pallas_call x2, Pallas kernels, block_work(): pl.pallas_call(functools.partial(work_kernel, first, last), grid=(NZ,), i...  18.2 us
    pallas_call x1, Pallas kernels, prepare(): pl.pallas_call(first_prep, grid=(steps,), in_specs=[whole, whole, point_s...  17 us
    pallas_call x1, Pallas kernels, prepare(): pl.pallas_call(later_prep, grid=(steps,), in_specs=[whole, point_spec], o...  12.5 us
    all_to_all x2, starting transfers between devices, exchange(): return lax.all_to_all(values, axes, split_axis=0, concat_axis=0, tiled=True)  9.84 us
    pallas_call x1, Pallas kernels, pick_back(): pl.pallas_call(return_kernel, grid=(npts // rows,), in_specs=[pl.BlockSpe...  9.63 us
  transfers between devices with their start and end apart: 6, of which 2 were waited for; matrix products, arithmetic and copies ran while one was open for 2% of the time, Pallas kernels for 19%

profile of v1, /device:TPU:1, one launch (start us, length us, event | category | flops | bytes accessed | tf_op | source)
XLA Modules:
  0.0 252.6 jit_solution(10076667761592331361)
XLA Ops:
  7.2 0.0 all-gather.3.cloned.1.call-start
  7.2 1.9 constant_dynamic-slice_fusion
  9.1 17.0 %shard_map.59 = (bf16[32,128,512]{2,1,0:T(8,128)(2,1)}, s32[1,2048]{1,0:T(1,128)}, s32[8,1,512]{2,1,0:T(1,128)}) custom-call(s32[1,2048]{1,0:T(1,128)} %bitcast.32, s32[1,2048]{1,0:T(1,128)} %bitcast.33, bf16[2048,1024]{1,0:T(8,128)(2,1)} %points_ref.3), custom_call_target="tpu_custom_call" | custom-call | flops 8589934592 | bytes 6291456 | tf_op jit(solution)/shard_map/pallas_call | solution.py:107
  26.1 15.5 %all_to_all.37 = s32[32,1,128]{2,1,0:T(1,128)S(1)} all-to-all(s32[32,1,128]{2,1,0:T(1,128)} %bitcast.30), channel_id=1, replica_groups=mesh['x'=4,'c'=2,'z'=8,'y'=4] {'x','c','y'}, dimensions={0} | all-to-all | bytes 32768 | tf_op jit(solution)/shard_map/all_to_all | solution.py:233
  41.6 5.1 %all-to-all-start.2 = ((bf16[32,128,512]{2,1,0:T(8,128)(2,1)}), bf16[32,128,512]{2,1,0:T(8,128)(2,1)}, u32[]{:S(2)}, u32[]{:S(2)}) async-start(bf16[32,128,512]{2,1,0:T(8,128)(2,1)} %get-tuple-element.11), calls=%async_computation.2 | async-start | bytes 8388608 | tf_op jit(solution)/shard_map/all_to_all | solution.py:233
  46.7 0.0 reduce-scatter.3.cloned.1.call-start
  46.7 0.1 copy.13
  46.8 0.1 copy.14
  46.9 0.7 reshape.61.refs_2_
  47.6 49.6 %all-to-all-done.2.refs_0_ = bf16[32,128,512]{2,1,0:T(8,128)(2,1)} async-done(((bf16[32,128,512]{2,1,0:T(8,128)(2,1)}), bf16[32,128,512]{2,1,0:T(8,128)(2,1)}, u32[]{:S(2)}, u32[]{:S(2)}) %all-to-all-start.2) | async-done | bytes 4194336 | tf_op jit(solution)/shard_map/all_to_all | solution.py:233
  97.2 8.9 %shard_map.61 = (bf16[8,264,512]{2,1,0:T(8,128)(2,1)}, f32[8,512,256]{2,1,0:T(8,128)}) custom-call(bf16[32,128,512]{2,1,0:T(8,128)(2,1)} %all-to-all-done.2.refs_0_, bf16[8,256,1024]{2,1,0:T(8,128)(2,1)} %bitcast.23, s32[8,1,512]{2,1,0:T(1,128)} %reshape.61.refs_2_), custom_call_target="tpu_custom_call" | custom-call | flops 2147483648 | bytes 16777216 | tf_op jit(solution)/shard_map/pallas_call | solution.py:186
  106.2 0.0 reduce-scatter.5.cloned.1.call-start
  106.2 12.5 %shard_map.60 = bf16[32,128,512]{2,1,0:T(8,128)(2,1)} custom-call(s32[1,2048]{1,0:T(1,128)} %get-tuple-element.9.slot_ref, bf16[2048,1024]{1,0:T(8,128)(2,1)} %points_ref.3), custom_call_target="tpu_custom_call" | custom-call | flops 8589934592 | bytes 6291456 | tf_op jit(solution)/shard_map/pallas_call | solution.py:99
  118.7 57.9 %all_to_all.38.refs_0_ = bf16[32,128,512]{2,1,0:T(8,128)(2,1)} all-to-all(bf16[32,128,512]{2,1,0:T(8,128)(2,1)} %shard_map.60), channel_id=1, replica_groups=mesh['x'=4,'c'=2,'z'=8,'y'=4] {'x','c','y'}, dimensions={0} | all-to-all | bytes 8388608 | tf_op jit(solution)/shard_map/all_to_all | solution.py:233
  176.6 9.3 %shard_map.62 = (bf16[8,256,512]{2,1,0:T(8,128)(2,1)}, bf16[32,128,256]{2,1,0:T(8,128)(2,1)}) custom-call(bf16[32,128,512]{2,1,0:T(8,128)(2,1)} %all_to_all.38.refs_0_, bf16[8,256,1024]{2,1,0:T(8,128)(2,1)} %bitcast.24, s32[8,1,512]{2,1,0:T(1,128)} %reshape.61.refs_2_, f32[8,512,256]{2,1,0:T(8,128)} %get-tuple-element.12.refs_3_), custom_call_target="tpu_custom_call" | custom-call | flops 2147483648 | bytes 16777216 | tf_op jit(solution)/shard_map/pallas_call | solution.py:186
  185.9 4.7 %all-to-all-start.3 = ((bf16[32,128,256]{2,1,0:T(8,128)(2,1)}), bf16[32,128,256]{2,1,0:T(8,128)(2,1)S(1)}, u32[]{:S(2)}, u32[]{:S(2)}) async-start(bf16[32,128,256]{2,1,0:T(8,128)(2,1)} %get-tuple-element.13), calls=%async_computation.3 | async-start | bytes 4194304 | tf_op jit(solution)/shard_map/all_to_all | solution.py:233
  190.7 0.0 reduce-scatter.3.cloned.1.call-done
  190.7 0.8 fusion.3
  191.5 1.0 slice_bitcast_fusion
  192.4 32.0 %reduce-scatter.5.cloned.1.call-done = bf16[1,256,512]{2,1,0:T(8,128)(2,1)} async-done(((bf16[8,256,512]{2,1,0:T(8,128)(2,1)}), bf16[1,256,512]{2,1,0:T(8,128)(2,1)}) %reduce-scatter.5.cloned.1.call-update) | async-done | bytes 262160 | tf_op jit(solution)/shard_map/reduce_scatter | solution.py:261
  224.4 2.1 copy_bitcast_fusion
  226.5 8.9 %all-to-all-start.4 = ((bf16[256,8,128]{2,0,1:T(8,128)(2,1)}), bf16[256,8,128]{2,0,1:T(8,128)(2,1)S(1)}, u32[]{:S(2)}, u32[]{:S(2)}) async-start(bf16[256,8,128]{2,0,1:T(8,128)(2,1)} %copy_bitcast_fusion), calls=%async_computation.6 | async-start | bytes 1048576 | tf_op jit(solution)/shard_map/all_to_all | solution.py:269
  235.4 9.6 %shard_map.63 = bf16[2048,256]{1,0:T(8,128)(2,1)} custom-call(s32[1,2048]{1,0:T(1,128)} %get-tuple-element.9.slot_ref, bf16[4096,256]{1,0:T(8,128)(2,1)} %bitcast.25), custom_call_target="tpu_custom_call" | custom-call | flops 4294967296 | bytes 3145728 | tf_op jit(solution)/shard_map/pallas_call | solution.py:215
  245.0 1.0 convert_element_type.49
  (8 shorter events, 0.1 us)
Async XLA Ops:
  7.2 90.1 %all-gather.3.cloned.1.call-start = ((), (), s32[]{:S(2)}) async-start(), calls=%async_computation.9 | async-start | bytes 4718592 | tf_op jit(solution)/shard_map/all_gather | solution.py:240
  41.6 55.7 %all-to-all-start.2 = ((bf16[32,128,512]{2,1,0:T(8,128)(2,1)}), bf16[32,128,512]{2,1,0:T(8,128)(2,1)}, u32[]{:S(2)}, u32[]{:S(2)}) async-start(bf16[32,128,512]{2,1,0:T(8,128)(2,1)} %get-tuple-element.11), calls=%async_computation.2 | async-start | bytes 8388608 | tf_op jit(solution)/shard_map/all_to_all | solution.py:233
  46.7 144.0 %reduce-scatter.3.cloned.1.call-start = ((), (), s32[]{:S(2)}) async-start(), calls=%async_computation.7 | async-start | bytes 2433024 | tf_op jit(solution)/shard_map/reduce_scatter | solution.py:261
  106.2 118.3 %reduce-scatter.5.cloned.1.call-start = ((), (), s32[]{:S(2)}) async-start(), calls=%async_computation.8 | async-start | bytes 2359296 | tf_op jit(solution)/shard_map/reduce_scatter | solution.py:261
  185.9 40.6 %all-to-all-start.3 = ((bf16[32,128,256]{2,1,0:T(8,128)(2,1)}), bf16[32,128,256]{2,1,0:T(8,128)(2,1)S(1)}, u32[]{:S(2)}, u32[]{:S(2)}) async-start(bf16[32,128,256]{2,1,0:T(8,128)(2,1)} %get-tuple-element.13), calls=%async_computation.3 | async-start | bytes 4194304 | tf_op jit(solution)/shard_map/all_to_all | solution.py:233
  226.5 8.9 %copy-start = (bf16[32,128,256]{2,1,0:T(8,128)(2,1)}, bf16[32,128,256]{2,1,0:T(8,128)(2,1)S(1)}, u32[]{:S(2)}) copy-start(bf16[32,128,256]{2,1,0:T(8,128)(2,1)S(1)} %all-to-all-done.3) | copy-start | bytes 6291460
  226.5 18.5 %all-to-all-start.4 = ((bf16[256,8,128]{2,0,1:T(8,128)(2,1)}), bf16[256,8,128]{2,0,1:T(8,128)(2,1)S(1)}, u32[]{:S(2)}, u32[]{:S(2)}) async-start(bf16[256,8,128]{2,0,1:T(8,128)(2,1)} %copy_bitcast_fusion), calls=%async_computation.6 | async-start | bytes 1048576 | tf_op jit(solution)/shard_map/all_to_all | solution.py:269
Sparse Core Ops, SparseCore 0:
  10.3 58.3 all-gather.2
  106.3 41.6 reduce-scatter.2
  186.1 38.3 reduce-scatter.4

commit v2 on v1

--- a/solution.py
+++ b/solution.py
@@ -23,10 +23,6 @@
 
 def nt_dot(a, b):
     return lax.dot_general(a, b, (((1,), (1,)), ((), ())), preferred_element_type=F32)
-
-
-def tn_dot(a, b):
-    return lax.dot_general(a, b, (((0,), (0,)), ((), ())), preferred_element_type=F32)
 
 
 def slots_of(block_row):
@@ -52,7 +48,28 @@
     return ((gg * NY + yy) * NZ + zz) * MOST + rank
 
 
-def first_prep(block_ref, final_ref, points_ref, out_ref, slot_ref, target_ref, slots):
+def pick_rows(slots, base, rows):
+    npts = slots.shape[1]
+    tall = 256
+    lane = 128
+    line = lax.broadcasted_iota(jnp.int32, (tall, lane), 0).astype(F32).astype(BF16)
+    parts = []
+    for i in range(rows // tall):
+        local = slots - (base + i * tall)
+        local = jnp.where((local >= 0) & (local < tall), local, -1).astype(F32).astype(BF16)
+        parts.append(
+            jnp.concatenate(
+                [
+                    jnp.where(line == local[:, k : k + lane], 1.0, 0.0).astype(BF16)
+                    for k in range(0, npts, lane)
+                ],
+                axis=1,
+            )
+        )
+    return jnp.concatenate(parts, axis=0)
+
+
+def first_prep(block_ref, final_ref, points_ref, out_ref, slot_ref, slots):
     step = pl.program_id(0)
 
     @pl.when(step == 0)
@@ -62,22 +79,21 @@
         slot_ref[...] = found
 
     rows = PER_STEP * SLOTS
-    npts = points_ref.shape[0]
-    at = step * rows + lax.broadcasted_iota(jnp.int32, (rows, npts), 0)
-    pick = jnp.where(at == slots[...], 1.0, 0.0).astype(BF16)
+    npts, width = points_ref.shape
+    pick = pick_rows(slots[...], step * rows, rows)
     moved = jnp.dot(pick, points_ref[...], preferred_element_type=F32)
-    out_ref[...] = moved.astype(BF16).reshape(out_ref.shape)
+    out_ref[:, 0:SLOTS] = moved.astype(BF16).reshape(PER_STEP, SLOTS, width)
     marks = jnp.broadcast_to((final_ref[...] + 1).astype(F32).astype(BF16), (8, npts))
-    target = nt_dot(marks, pick)[0:1] - 1.0
-    target_ref[...] = target.astype(jnp.int32).reshape(target_ref.shape)
+    target = nt_dot(marks, pick).astype(BF16)
+    blank = jnp.zeros((8, width - SLOTS), BF16)
+    for i in range(PER_STEP):
+        one = target[:, i * SLOTS : (i + 1) * SLOTS]
+        out_ref[i, SLOTS : SLOTS + 8] = jnp.concatenate([one, blank], axis=1)
 
 
 def later_prep(slot_ref, points_ref, out_ref):
-    step = pl.program_id(0)
     rows = PER_STEP * SLOTS
-    npts = points_ref.shape[0]
-    at = step * rows + lax.broadcasted_iota(jnp.int32, (rows, npts), 0)
-    pick = jnp.where(at == slot_ref[...], 1.0, 0.0).astype(BF16)
+    pick = pick_rows(slot_ref[...], pl.program_id(0) * rows, rows)
     moved = jnp.dot(pick, points_ref[...], preferred_element_type=F32)
     out_ref[...] = moved.astype(BF16).reshape(out_ref.shape)
 
@@ -88,8 +104,9 @@
     column = start // width
     whole = pl.BlockSpec((1, npts), lambda i: (0, 0))
     point_spec = pl.BlockSpec((npts, width), lambda i: (0, column))
-    out_spec = pl.BlockSpec((PER_STEP, SLOTS, width), lambda i: (i, 0, 0))
-    out_shape = jax.ShapeDtypeStruct((DESTS, SLOTS, width), BF16)
+    tall = SLOTS if slot_row is not None else SLOTS + 8
+    out_spec = pl.BlockSpec((PER_STEP, tall, width), lambda i: (i, 0, 0))
+    out_shape = jax.ShapeDtypeStruct((DESTS, tall, width), BF16)
     cost = pl.CostEstimate(
         flops=2 * DESTS * SLOTS * npts * width,
         bytes_accessed=2 * width * (npts + DESTS * SLOTS),
@@ -108,16 +125,8 @@
         first_prep,
         grid=(steps,),
         in_specs=[whole, whole, point_spec],
-        out_specs=(
-            out_spec,
-            whole,
-            pl.BlockSpec((1, 1, PER_STEP * SLOTS), lambda i: (i, 0, 0)),
-        ),
-        out_shape=(
-            out_shape,
-            jax.ShapeDtypeStruct((1, npts), jnp.int32),
-            jax.ShapeDtypeStruct((steps, 1, PER_STEP * SLOTS), jnp.int32),
-        ),
+        out_specs=(out_spec, whole),
+        out_shape=(out_shape, jax.ShapeDtypeStruct((1, npts), jnp.int32)),
         scratch_shapes=[pltpu.VMEM((1, npts), jnp.int32)],
         cost_estimate=cost,
     )(block_row, final_row, points)
@@ -234,37 +243,33 @@
 
 
 def shards(points, blocks, finals, centroids):
-    npts, width = points.shape
+    npts, _ = points.shape
     group = lax.axis_index("x") * NC + lax.axis_index("c")
     own = lax.dynamic_slice_in_dim(centroids, group * BS, BS, 0)
     table = lax.all_gather(own, "z", axis=0, tiled=False)
 
     block_row = blocks.reshape(1, npts)
     final_row = finals.reshape(1, npts)
-    slot_row = None
-    arrived, start = [], 0
-    for size in WIDTHS:
-        if slot_row is None:
-            sent, slot_row, target = prepare(block_row, final_row, points, start, size, None)
-            arrived.append(exchange(sent, PLANE))
-            target = exchange(target.reshape(DESTS, SLOTS), PLANE)
-            target = jnp.transpose(target.reshape(DESTS, NZ, MOST), (1, 0, 2))
-            target = target.reshape(NZ, 1, DESTS * MOST)
-        else:
-            sent = prepare(block_row, final_row, points, start, size, slot_row)
-            arrived.append(exchange(sent, PLANE))
-        start += size
-
-    part, start, shares = None, 0, []
-    for i, size in enumerate(WIDTHS):
-        sums, part = block_work(arrived[i], table, target, part, start, i == len(WIDTHS) - 1)
-        shares.append(lax.psum_scatter(sums, "z", scatter_dimension=0, tiled=True)[0])
-        start += size
+    low, high = WIDTHS
+    sent, slot_row = prepare(block_row, final_row, points, 0, low, None)
+    here = exchange(sent, PLANE)
+    later = prepare(block_row, final_row, points, low, high, slot_row)
+    here, later = lax.optimization_barrier((here, later))
+    then = exchange(later, PLANE)
+
+    target = here[:, SLOTS, :SLOTS].astype(jnp.int32) - 1
+    target = jnp.transpose(target.reshape(DESTS, NZ, MOST), (1, 0, 2))
+    target = target.reshape(NZ, 1, DESTS * MOST)
+    sums, part = block_work(here, table, target, None, 0, False)
+    share = lax.psum_scatter(sums, "z", scatter_dimension=0, tiled=True)[0]
+    more, part = block_work(then, table, target, part, low, True)
+    rest = lax.psum_scatter(more, "z", scatter_dimension=0, tiled=True)[0]
     returned = exchange(part, PLANE).reshape(DESTS * SLOTS, BS)
     distances = pick_back(slot_row, returned)
-
-    counts = shares[0][BS, :BS].astype(F32) + 16.0 * shares[0][BS + 1, :BS].astype(F32)
-    total = jnp.concatenate([s[:BS].astype(F32) for s in shares], axis=1)
+    distances, rest = lax.optimization_barrier((distances, rest))
+
+    counts = share[BS, :BS].astype(F32) + 16.0 * share[BS + 1, :BS].astype(F32)
+    total = jnp.concatenate([share[:BS].astype(F32), rest.astype(F32)], axis=1)
     fresh = (total + own.astype(F32)) / (counts + 1.0)[:, None]
     fresh = lax.all_to_all(fresh.astype(BF16), ("x", "c"), split_axis=1, concat_axis=0, tiled=True)
     return distances, fresh.astype(F32)

time: 254 us -> 234 us (0.921)
  waiting for transfers between devices: 81.6 us -> 40.9 us
  blocking collectives: 73.4 us -> 104 us
  starting transfers between devices: 18.8 us -> 8.72 us
    reduce_scatter x2, waiting for transfers between devices: 32 us -> 0.02 us  [the longest x1 0.02 us: shards(): rest = lax.psum_scatter(more, 'z', scatter_dimension=0, tiled=True)[0]]
    all_to_all x2, blocking collectives: 73.4 us -> 91.2 us  [exchange(): return lax.all_to_all(values, axes, split_axis=0, concat_axis=0, tiled=True)]
    all_to_all x0 -> x1, blocking collectives: none -> 13.1 us  [shards(): lax.all_to_all(fresh.astype(BF16), ('x', 'c'), split_axis=1, concat_axis=...]
    all_to_all x1 -> x0, starting transfers between devices: 8.86 us -> none  [shards(): lax.all_to_all(fresh.astype(BF16), ('x', 'c'), split_axis=1, concat_axis=...]
    all_to_all x2 -> x1, waiting for transfers between devices: 49.6 us -> 40.8 us  [exchange(): return lax.all_to_all(values, axes, split_axis=0, concat_axis=0, tiled=True)]
    all_to_all x2 -> x1, starting transfers between devices: 9.84 us -> 8.6 us  [exchange(): return lax.all_to_all(values, axes, split_axis=0, concat_axis=0, tiled=True)]
  transfers between devices with their start and end apart: 6 -> 4, of which waited for: 2 -> 1; matrix products, arithmetic and copies ran while one was open for 2% -> 2% of each run, Pallas kernels for 19% -> 21%
where the time goes in v2:
time: 234 us; the launch traced here: 233 us
  blocking collectives  104 us (44%)
  Pallas kernels  57.9 us (25%)
  waiting for transfers between devices  40.9 us (17%)
  between operations  13.8 us (6%)
  starting transfers between devices  8.72 us (4%)
  other arithmetic  4 us (2%)
  local copies, waits for them, and re-layouts  3.75 us (2%)
    all_to_all x2, blocking collectives, exchange(): return lax.all_to_all(values, axes, split_axis=0, concat_axis=0, tiled=True)  91.2 us
    all_to_all x1, waiting for transfers between devices, exchange(): return lax.all_to_all(values, axes, split_axis=0, concat_axis=0, tiled=True)  40.8 us
    pallas_call x2, Pallas kernels, block_work(): pl.pallas_call(functools.partial(work_kernel, first, last), grid=(NZ,), i...  18.3 us
    pallas_call x1, Pallas kernels, prepare(): pl.pallas_call(first_prep, grid=(steps,), in_specs=[whole, whole, point_s...  17.3 us
    all_to_all x1, blocking collectives, shards(): lax.all_to_all(fresh.astype(BF16), ('x', 'c'), split_axis=1, concat_axis=...  13.1 us
    pallas_call x1, Pallas kernels, prepare(): pl.pallas_call(later_prep, grid=(steps,), in_specs=[whole, point_spec], o...  12.7 us
    pallas_call x1, Pallas kernels, pick_back(): pl.pallas_call(return_kernel, grid=(npts // rows,), in_specs=[pl.BlockSpe...  9.64 us
    all_to_all x1, starting transfers between devices, exchange(): return lax.all_to_all(values, axes, split_axis=0, concat_axis=0, tiled=True)  8.6 us
  transfers between devices with their start and end apart: 4, of which 1 were waited for; matrix products, arithmetic and copies ran while one was open for 2% of the time, Pallas kernels for 21%

profile of v2, /device:TPU:1, one launch (start us, length us, event | category | flops | bytes accessed | tf_op | source)
XLA Modules:
  0.0 233.3 jit_solution(7215909192029189676)
XLA Ops:
  7.2 0.0 all-gather.3.cloned.1.call-start
  7.2 1.9 constant_dynamic-slice_fusion
  9.1 0.0 all-gather.3.cloned.1.call-update
  9.1 17.3 %shard_map.59 = (bf16[32,136,512]{2,1,0:T(8,128)(2,1)}, s32[1,2048]{1,0:T(1,128)}) custom-call(s32[1,2048]{1,0:T(1,128)} %bitcast.28, s32[1,2048]{1,0:T(1,128)} %bitcast.29, bf16[2048,1024]{1,0:T(8,128)(2,1)} %points_ref.3), custom_call_target="tpu_custom_call" | custom-call | flops 8589934592 | bytes 6291456 | tf_op jit(solution)/shard_map/pallas_call | solution.py:124
  26.4 8.6 %all-to-all-start = ((bf16[32,136,512]{2,1,0:T(8,128)(2,1)}), bf16[32,136,512]{2,1,0:T(8,128)(2,1)}, u32[]{:S(2)}, u32[]{:S(2)}) async-start(bf16[32,136,512]{2,1,0:T(8,128)(2,1)} %get-tuple-element.13), calls=%async_computation | async-start | bytes 8912896 | tf_op jit(solution)/shard_map/all_to_all | solution.py:242
  35.0 0.0 reduce-scatter.5.cloned.1.call-start
  35.1 12.7 %shard_map.60 = bf16[32,128,512]{2,1,0:T(8,128)(2,1)} custom-call(s32[1,2048]{1,0:T(1,128)} %get-tuple-element.12.slot_ref, bf16[2048,1024]{1,0:T(8,128)(2,1)} %points_ref.3), custom_call_target="tpu_custom_call" | custom-call | flops 8589934592 | bytes 6291456 | tf_op jit(solution)/shard_map/pallas_call | solution.py:116
  47.7 40.8 %all-to-all-done.refs_0_ = bf16[32,136,512]{2,1,0:T(8,128)(2,1)} async-done(((bf16[32,136,512]{2,1,0:T(8,128)(2,1)}), bf16[32,136,512]{2,1,0:T(8,128)(2,1)}, u32[]{:S(2)}, u32[]{:S(2)}) %all-to-all-start) | async-done | bytes 4456480 | tf_op jit(solution)/shard_map/all_to_all | solution.py:242
  88.6 0.9 convert_add_fusion
  89.4 0.1 copy.18
  89.5 0.1 copy.19
  89.6 0.7 reshape.55.refs_2_
  90.3 9.0 %shard_map.61 = (bf16[8,264,512]{2,1,0:T(8,128)(2,1)}, f32[8,512,256]{2,1,0:T(8,128)}) custom-call(bf16[32,136,512]{2,1,0:T(8,128)(2,1)} %all-to-all-done.refs_0_, bf16[8,256,1024]{2,1,0:T(8,128)(2,1)} %bitcast.20, s32[8,1,512]{2,1,0:T(1,128)} %reshape.55.refs_2_), custom_call_target="tpu_custom_call" | custom-call | flops 2147483648 | bytes 16777216 | tf_op jit(solution)/shard_map/pallas_call | solution.py:195
  99.3 0.0 reduce-scatter.3.cloned.1.call-start
  99.4 58.1 %all_to_all.28.refs_0_ = bf16[32,128,512]{2,1,0:T(8,128)(2,1)} all-to-all(bf16[32,128,512]{2,1,0:T(8,128)(2,1)} %shard_map.60), channel_id=1, replica_groups=mesh['x'=4,'c'=2,'z'=8,'y'=4] {'x','c','y'}, dimensions={0} | all-to-all | bytes 8388608 | tf_op jit(solution)/shard_map/all_to_all | solution.py:242
  157.5 9.3 %shard_map.62 = (bf16[8,256,512]{2,1,0:T(8,128)(2,1)}, bf16[32,128,256]{2,1,0:T(8,128)(2,1)}) custom-call(bf16[32,128,512]{2,1,0:T(8,128)(2,1)} %all_to_all.28.refs_0_, bf16[8,256,1024]{2,1,0:T(8,128)(2,1)} %bitcast.21, s32[8,1,512]{2,1,0:T(1,128)} %reshape.55.refs_2_, f32[8,512,256]{2,1,0:T(8,128)} %get-tuple-element.16.refs_3_), custom_call_target="tpu_custom_call" | custom-call | flops 2147483648 | bytes 16777216 | tf_op jit(solution)/shard_map/pallas_call | solution.py:195
  166.8 33.0 %all_to_all.29 = bf16[32,128,256]{2,1,0:T(8,128)(2,1)} all-to-all(bf16[32,128,256]{2,1,0:T(8,128)(2,1)} %get-tuple-element.17), channel_id=1, replica_groups=mesh['x'=4,'c'=2,'z'=8,'y'=4] {'x','c','y'}, dimensions={0} | all-to-all | bytes 4194304 | tf_op jit(solution)/shard_map/all_to_all | solution.py:242
  199.9 9.6 %shard_map.63 = bf16[2048,256]{1,0:T(8,128)(2,1)} custom-call(s32[1,2048]{1,0:T(1,128)} %get-tuple-element.12.slot_ref, bf16[4096,256]{1,0:T(8,128)(2,1)} %bitcast.22), custom_call_target="tpu_custom_call" | custom-call | flops 4294967296 | bytes 3145728 | tf_op jit(solution)/shard_map/pallas_call | solution.py:224
  209.5 0.8 fusion.3
  210.3 1.0 slice_bitcast_fusion
  211.3 0.0 reduce-scatter.3.cloned.1.call-done
  211.3 1.3 copy_bitcast_fusion
  212.6 13.1 %all_to_all.30 = bf16[256,8,128]{2,0,1:T(8,128)(2,1)S(1)} all-to-all(bf16[256,8,128]{2,0,1:T(8,128)(2,1)S(1)} %copy_bitcast_fusion), channel_id=1, replica_groups=mesh['x'=4,'c'=2,'z'=8,'y'=4] {'x','c'}, dimensions={1} | all-to-all | bytes 1048576 | tf_op jit(solution)/shard_map/all_to_all | solution.py:274
  225.7 1.0 convert_element_type.51
  (4 shorter events, 0.0 us)
Async XLA Ops:
  7.2 83.2 %all-gather.3.cloned.1.call-start = ((), (), s32[]{:S(2)}) async-start(), calls=%async_computation.8 | async-start | bytes 4718592 | tf_op jit(solution)/shard_map/all_gather | solution.py:249
  26.4 62.1 %all-to-all-start = ((bf16[32,136,512]{2,1,0:T(8,128)(2,1)}), bf16[32,136,512]{2,1,0:T(8,128)(2,1)}, u32[]{:S(2)}, u32[]{:S(2)}) async-start(bf16[32,136,512]{2,1,0:T(8,128)(2,1)} %get-tuple-element.13), calls=%async_computation | async-start | bytes 8912896 | tf_op jit(solution)/shard_map/all_to_all | solution.py:242
  35.0 174.5 %reduce-scatter.5.cloned.1.call-start = ((), (), s32[]{:S(2)}) async-start(), calls=%async_computation.7 | async-start | bytes 2433024 | tf_op jit(solution)/shard_map/reduce_scatter | solution.py:264
  99.3 112.0 %reduce-scatter.3.cloned.1.call-start = ((), (), s32[]{:S(2)}) async-start(), calls=%async_computation.6 | async-start | bytes 2359296 | tf_op jit(solution)/shard_map/reduce_scatter | solution.py:266
Sparse Core Ops, SparseCore 0:
  10.3 58.3 all-gather.2
  99.5 41.8 reduce-scatter.4
  167.0 38.2 reduce-scatter.2

commit v3 on v2

v3 whole, which is shorter than its diff:
```python
import functools

import jax
import jax.numpy as jnp
from jax import lax
from jax.experimental import pallas as pl
from jax.experimental.pallas import tpu as pltpu
from jax.sharding import Mesh
from jax.sharding import PartitionSpec as P

BS = 256
MOST = 16
NX, NC, NZ, NY = 4, 2, 8, 4
NG = NX * NC
NB = NZ * NY * NG
DESTS = NG * NY
SLOTS = NZ * MOST
WIDTHS = (768, 256)
PLANE = ("x", "c", "y")
DIGIT = 64
PER_STEP = 4
F32, BF16 = jnp.float32, jnp.bfloat16


def nt_dot(a, b):
    return lax.dot_general(a, b, (((1,), (1,)), ((), ())), preferred_element_type=F32)


def slots_of(block_row):
    npts = block_row.shape[1]
    piece = 128
    row = lax.broadcasted_iota(jnp.int32, (piece, 2 * piece), 0)
    column = lax.broadcasted_iota(jnp.int32, (piece, 2 * piece), 1)
    before = jnp.where((row < column) | (column >= piece), 1.0, 0.0).astype(BF16)
    carry = jnp.zeros((NB, piece), F32)
    ranks = []
    for i in range(npts // piece):
        part = block_row[:, i * piece : (i + 1) * piece]
        member = lax.broadcasted_iota(jnp.int32, (NB, piece), 0) == part
        ones = jnp.where(member, 1.0, 0.0)
        seen = jnp.dot(ones.astype(BF16), before, preferred_element_type=F32)
        ranks.append(jnp.sum(ones * (seen[:, :piece] + carry), axis=0, keepdims=True))
        carry = carry + seen[:, piece:]
    rank = jnp.concatenate(ranks, axis=1).astype(jnp.int32)
    zz = block_row // (NY * NG)
    yy = (block_row // NG) % NY
    gg = block_row % NG
    return ((gg * NY + yy) * NZ + zz) * MOST + rank


def low_digits(slots):
    line = lax.broadcasted_iota(jnp.int32, (DIGIT, slots.shape[1]), 0)
    return jnp.where(line == slots % DIGIT, 1.0, 0.0).astype(BF16)


def pick_rows(slots, low, base, rows):
    npts = slots.shape[1]
    line = lax.broadcasted_iota(jnp.int32, (rows // DIGIT, npts), 0)
    high = jnp.where(line + base // DIGIT == slots // DIGIT, 1.0, 0.0)
    parts = []
    for i in range(rows // DIGIT):
        one = jnp.broadcast_to(high[i : i + 1], (16, npts)).astype(BF16)
        parts.append(low * jnp.concatenate([one] * (DIGIT // 16), axis=0))
    return jnp.concatenate(parts, axis=0)


def first_prep(block_ref, final_ref, points_ref, out_ref, slot_ref, slots, low):
    step = pl.program_id(0)

    @pl.when(step == 0)
    def _():
        found = slots_of(block_ref[...])
        slots[...] = found
        slot_ref[...] = found
        low[...] = low_digits(found)

    rows = PER_STEP * SLOTS
    npts, width = points_ref.shape
    pick = pick_rows(slots[...], low[...], step * rows, rows)
    moved = jnp.dot(pick, points_ref[...], preferred_element_type=F32)
    out_ref[:, 0:SLOTS] = moved.astype(BF16).reshape(PER_STEP, SLOTS, width)
    marks = jnp.broadcast_to((final_ref[...] + 1).astype(F32).astype(BF16), (8, npts))
    target = nt_dot(marks, pick).astype(BF16)
    blank = jnp.zeros((8, width - SLOTS), BF16)
    for i in range(PER_STEP):
        one = target[:, i * SLOTS : (i + 1) * SLOTS]
        out_ref[i, SLOTS : SLOTS + 8] = jnp.concatenate([one, blank], axis=1)


def later_prep(slot_ref, points_ref, out_ref, low):
    step = pl.program_id(0)

    @pl.when(step == 0)
    def _():
        low[...] = low_digits(slot_ref[...])

    rows = PER_STEP * SLOTS
    pick = pick_rows(slot_ref[...], low[...], step * rows, rows)
    moved = jnp.dot(pick, points_ref[...], preferred_element_type=F32)
    out_ref[...] = moved.astype(BF16).reshape(out_ref.shape)


def prepare(block_row, final_row, points, start, width, slot_row):
    npts = points.shape[0]
    steps = DESTS // PER_STEP
    column = start // width
    whole = pl.BlockSpec((1, npts), lambda i: (0, 0))
    point_spec = pl.BlockSpec((npts, width), lambda i: (0, column))
    tall = SLOTS if slot_row is not None else SLOTS + 8
    out_spec = pl.BlockSpec((PER_STEP, tall, width), lambda i: (i, 0, 0))
    out_shape = jax.ShapeDtypeStruct((DESTS, tall, width), BF16)
    cost = pl.CostEstimate(
        flops=2 * DESTS * SLOTS * npts * width,
        bytes_accessed=2 * width * (npts + DESTS * SLOTS),
        transcendentals=0,
    )
    if slot_row is not None:
        return pl.pallas_call(
            later_prep,
            grid=(steps,),
            in_specs=[whole, point_spec],
            out_specs=out_spec,
            out_shape=out_shape,
            scratch_shapes=[pltpu.VMEM((DIGIT, npts), BF16)],
            cost_estimate=cost,
        )(slot_row, points)
    return pl.pallas_call(
        first_prep,
        grid=(steps,),
        in_specs=[whole, whole, point_spec],
        out_specs=(out_spec, whole),
        out_shape=(out_shape, jax.ShapeDtypeStruct((1, npts), jnp.int32)),
        scratch_shapes=[pltpu.VMEM((1, npts), jnp.int32), pltpu.VMEM((DIGIT, npts), BF16)],
        cost_estimate=cost,
    )(block_row, final_row, points)


def work_kernel(first, me_ref, *refs):
    del me_ref
    place = pl.program_id(0)
    rows_ref, cent_ref, target_ref = refs[:3]
    rows = rows_ref[...].reshape(DESTS * MOST, rows_ref.shape[-1])
    table = cent_ref[0]
    onehot = jnp.where(
        lax.broadcasted_iota(jnp.int32, (BS, DESTS * MOST), 0) == target_ref[0], 1.0, 0.0
    ).astype(BF16)
    sums = jnp.dot(onehot, rows, preferred_element_type=F32).astype(BF16)
    cross = nt_dot(rows, table)
    wide = rows.astype(F32)
    row_norm = jnp.sum(wide * wide, axis=1, keepdims=True)
    tall = table.astype(F32)
    cent_norm = jnp.sum(tall * tall, axis=1, keepdims=True)
    cent_norm = jnp.transpose(jnp.broadcast_to(cent_norm, (BS, 128)))[0:1]
    total = row_norm - 2.0 * cross + cent_norm
    if first:
        sums_ref, result_ref = refs[3:]
        sums_ref[0, 0:BS] = sums
        ones = jnp.ones((8, DESTS * MOST), BF16)
        count = nt_dot(ones, onehot)
        high = jnp.floor(count * (1.0 / 16.0))
        low = count - 16.0 * high
        which = lax.broadcasted_iota(jnp.int32, count.shape, 0)
        digits = jnp.where(which == 0, low, jnp.where(which == 1, high, 0.0))
        blank = jnp.zeros((8, sums.shape[1] - BS), F32)
        digits = jnp.concatenate([digits, blank], axis=1)
        sums_ref[0, BS : BS + 8] = digits.astype(BF16)
        result_ref[0] = total
    else:
        part_ref, sum_refs, result_ref = refs[3], refs[4:-1], refs[-1]
        for i in range(NZ):

            @pl.when(place == i)
            def _(i=i):
                sum_refs[i][...] = sums

        total = (total + part_ref[0]) * (1.0 / 1024.0)
        result_ref[...] = total.astype(BF16).reshape(result_ref.shape)


def block_work(me, rows, table, target, part, start):
    width = rows.shape[-1]
    first = part is None
    taken = DESTS * MOST
    away = lambda k, me: lax.rem(me[0] - k + NZ, NZ)
    part_spec = pl.BlockSpec((1, taken, BS), lambda k, me: (k, 0, 0))
    row_spec = pl.BlockSpec((DESTS, MOST, width), lambda k, me: (0, away(k, me), 0))
    in_specs = [
        row_spec,
        pl.BlockSpec((1, BS, width), lambda k, me: (away(k, me), 0, start // width)),
        pl.BlockSpec((1, 1, taken), lambda k, me: (away(k, me), 0, 0)),
    ]
    operands = [rows, table, target]
    if first:
        out_specs = (
            pl.BlockSpec((1, BS + 8, width), lambda k, me: (away(k, me), 0, 0)),
            part_spec,
        )
        out_shape = (
            jax.ShapeDtypeStruct((NZ, BS + 8, width), BF16),
            jax.ShapeDtypeStruct((NZ, taken, BS), F32),
        )
    else:
        in_specs.append(part_spec)
        operands.append(part)
        out_specs = (pl.BlockSpec((BS, width), lambda k, me: (0, 0)),) * NZ + (
            pl.BlockSpec((DESTS, MOST, BS), lambda k, me: (0, away(k, me), 0)),
        )
        out_shape = (jax.ShapeDtypeStruct((BS, width), BF16),) * NZ + (
            jax.ShapeDtypeStruct((DESTS, SLOTS, BS), BF16),
        )
    return pl.pallas_call(
        functools.partial(work_kernel, first),
        grid_spec=pltpu.PrefetchScalarGridSpec(
            num_scalar_prefetch=1,
            grid=(NZ,),
            in_specs=in_specs,
            out_specs=out_specs,
        ),
        out_shape=out_shape,
        cost_estimate=pl.CostEstimate(
            flops=4 * NZ * taken * BS * width,
            bytes_accessed=2 * width * NZ * (taken + 2 * BS) + 8 * NZ * taken * BS,
            transcendentals=0,
        ),
    )(me, *operands)


def return_kernel(slot_ref, returned_ref, out_ref):
    rows = out_ref.shape[0]
    total = returned_ref.shape[0]
    slot = jnp.broadcast_to(slot_ref[...].astype(F32), (128, rows))
    column = jnp.transpose(slot)[:, 0:1].astype(jnp.int32)
    pick = jnp.where(
        lax.broadcasted_iota(jnp.int32, (rows, total), 1) == column, 1.0, 0.0
    ).astype(BF16)
    got = jnp.dot(pick, returned_ref[...], preferred_element_type=F32)
    out_ref[...] = got.astype(BF16)


def pick_back(slot_row, returned):
    npts = slot_row.shape[1]
    rows = 256
    return pl.pallas_call(
        return_kernel,
        grid=(npts // rows,),
        in_specs=[
            pl.BlockSpec((1, rows), lambda i: (0, i)),
            pl.BlockSpec(returned.shape, lambda i: (0, 0)),
        ],
        out_specs=pl.BlockSpec((rows, BS), lambda i: (i, 0)),
        out_shape=jax.ShapeDtypeStruct((npts, BS), BF16),
        cost_estimate=pl.CostEstimate(
            flops=2 * npts * returned.shape[0] * BS,
            bytes_accessed=2 * BS * (npts + returned.shape[0]),
            transcendentals=0,
        ),
    )(slot_row, returned)


def exchange(values, axes):
    return lax.all_to_all(values, axes, split_axis=0, concat_axis=0, tiled=True)


def sum_over_planes(sums):
    total = sums[0].astype(F32)
    for k in sorted(range(1, NZ), key=lambda k: -min(k, NZ - k)):
        got = lax.ppermute(sums[k], "z", [(i, (i - k) % NZ) for i in range(NZ)])
        total = total + got.astype(F32)
    return total


def shards(points, blocks, finals, centroids):
    npts, _ = points.shape
    group = lax.axis_index("x") * NC + lax.axis_index("c")
    me = lax.axis_index("z").astype(jnp.int32).reshape(1)
    own = lax.dynamic_slice_in_dim(centroids, group * BS, BS, 0)
    table = lax.all_gather(own, "z", axis=0, tiled=False)

    block_row = blocks.reshape(1, npts)
    final_row = finals.reshape(1, npts)
    cut = WIDTHS[0]
    sent, slot_row = prepare(block_row, final_row, points, 0, cut, None)
    here = exchange(sent, PLANE)
    sent = prepare(block_row, final_row, points, cut, WIDTHS[1], slot_row)
    then = exchange(sent, PLANE)
    target = here[:, SLOTS, :SLOTS].astype(jnp.int32) - 1
    target = jnp.transpose(target.reshape(DESTS, NZ, MOST), (1, 0, 2))
    target = target.reshape(NZ, 1, DESTS * MOST)
    sums, part = block_work(me, here, table, target, None, 0)
    share = lax.psum_scatter(sums, "z", scatter_dimension=0, tiled=True)[0]
    *rest, part = block_work(me, then, table, target, part, cut)
    returned = exchange(part, PLANE).reshape(DESTS * SLOTS, BS)
    rest = sum_over_planes(rest)
    distances = pick_back(slot_row, returned)

    counts = share[BS, :BS].astype(F32) + 16.0 * share[BS + 1, :BS].astype(F32)
    total = jnp.concatenate([share[:BS].astype(F32), rest], axis=1)
    fresh = (total + own.astype(F32)) / (counts + 1.0)[:, None]
    fresh = lax.all_to_all(
        fresh.astype(BF16), ("x", "c"), split_axis=1, concat_axis=0, tiled=True
    )
    return distances, fresh.astype(F32)


def solution(mesh):
    split = Mesh(mesh.devices.reshape(NX, NC, NZ, NY), ("x", "c", "z", "y"))
    every = ("x", "c", "z", "y")
    placed = (P(every, None), P(every, None), P(every), P(("z", "y"), None))
    return jax.shard_map(
        shards,
        mesh=split,
        in_specs=placed,
        out_specs=(P(every, None), P(("z", "y"), ("x", "c"))),
        check_vma=False,
    )
```

time: 234 us -> 252 us (1.077)
  blocking collectives: 104 us -> 34.9 us
  waiting for transfers between devices: 40.9 us -> 95.5 us
  starting transfers between devices: 8.72 us -> 38.1 us
    all_to_all x2 -> x1, blocking collectives: 91.2 us -> 34.9 us  [exchange(): return lax.all_to_all(values, axes, split_axis=0, concat_axis=0, tiled=True)]
    all_to_all x1 -> x2, waiting for transfers between devices: 40.8 us -> 83.4 us  [exchange(): return lax.all_to_all(values, axes, split_axis=0, concat_axis=0, tiled=True)]
    ppermute x0 -> x7, starting transfers between devices: none -> 18.8 us  [sum_over_planes(): got = lax.ppermute(sums[k], 'z', [(i, (i - k) % NZ) for i in range(NZ)])]
    all_to_all x1 -> x0, blocking collectives: 13.1 us -> none  [shards(): lax.all_to_all(fresh.astype(BF16), ('x', 'c'), split_axis=1, concat_axis=...]
    ppermute x0 -> x7, waiting for transfers between devices: none -> 12 us  [sum_over_planes(): got = lax.ppermute(sums[k], 'z', [(i, (i - k) % NZ) for i in range(NZ)])]
    all_to_all x0 -> x1, starting transfers between devices: none -> 5.7 us  [shards(): lax.all_to_all(fresh.astype(BF16), ('x', 'c'), split_axis=1, concat_axis=...]
    pallas_call x1, Pallas kernels: 17.3 us -> 22.6 us  [prepare(): pl.pallas_call(first_prep, grid=(steps,), in_specs=[whole, whole, point_s...]
    all_to_all x1 -> x2, starting transfers between devices: 8.6 us -> 13.5 us  [exchange(): return lax.all_to_all(values, axes, split_axis=0, concat_axis=0, tiled=True)]
  transfers between devices with their start and end apart: 4 -> 12, of which waited for: 1 -> 5; matrix products, arithmetic and copies ran while one was open for 2% -> 2% of each run, Pallas kernels for 21% -> 19%
where the time goes in v3:
time: 252 us; the launch traced here: 251 us
  waiting for transfers between devices  95.5 us (38%)
  Pallas kernels  59.5 us (24%)
  starting transfers between devices  38.1 us (15%)
  blocking collectives  34.9 us (14%)
  between operations  14.2 us (6%)
  other arithmetic  5.88 us (2%)
  local copies, waits for them, and re-layouts  2.83 us (1%)
    all_to_all x2, waiting for transfers between devices, exchange(): return lax.all_to_all(values, axes, split_axis=0, concat_axis=0, tiled=True)  83.4 us
    all_to_all x1, blocking collectives, exchange(): return lax.all_to_all(values, axes, split_axis=0, concat_axis=0, tiled=True)  34.9 us
    pallas_call x1, Pallas kernels, prepare(): pl.pallas_call(first_prep, grid=(steps,), in_specs=[whole, whole, point_s...  22.6 us
    pallas_call x2, Pallas kernels, block_work(): pl.pallas_call(functools.partial(work_kernel, first), grid_spec=pltpu.Pre...  19.4 us
    ppermute x7, starting transfers between devices, sum_over_planes(): got = lax.ppermute(sums[k], 'z', [(i, (i - k) % NZ) for i in range(NZ)])  18.8 us
    all_to_all x2, starting transfers between devices, exchange(): return lax.all_to_all(values, axes, split_axis=0, concat_axis=0, tiled=True)  13.5 us
    ppermute x7, waiting for transfers between devices, sum_over_planes(): got = lax.ppermute(sums[k], 'z', [(i, (i - k) % NZ) for i in range(NZ)])  12 us
    pallas_call x1, Pallas kernels, pick_back(): pl.pallas_call(return_kernel, grid=(npts // rows,), in_specs=[pl.BlockSpe...  9.63 us
  transfers between devices with their start and end apart: 12, of which 5 were waited for; matrix products, arithmetic and copies ran while one was open for 2% of the time, Pallas kernels for 19%

profile of v3, /device:TPU:1, one launch (start us, length us, event | category | flops | bytes accessed | tf_op | source)
XLA Modules:
  0.0 250.9 jit_solution(3552357112073532650)
XLA Ops:
  7.2 1.9 constant_dynamic-slice_fusion
  9.1 22.6 %shard_map.59 = (bf16[32,136,768]{2,1,0:T(8,128)(2,1)}, s32[1,2048]{1,0:T(1,128)}) custom-call(s32[1,2048]{1,0:T(1,128)} %bitcast.30, s32[1,2048]{1,0:T(1,128)} %bitcast.31, bf16[2048,1024]{1,0:T(8,128)(2,1)} %points_ref.3), custom_call_target="tpu_custom_call" | custom-call | flops 12884901888 | bytes 9437184 | tf_op jit(solution)/shard_map/pallas_call | solution.py:127
  31.8 8.6 %all-to-all-start.1 = ((bf16[32,136,768]{2,1,0:T(8,128)(2,1)}), bf16[32,136,768]{2,1,0:T(8,128)(2,1)}, u32[]{:S(2)}, u32[]{:S(2)}) async-start(bf16[32,136,768]{2,1,0:T(8,128)(2,1)} %get-tuple-element.16), calls=%async_computation.1 | async-start | bytes 13369344 | tf_op jit(solution)/shard_map/all_to_all | solution.py:261
  40.5 83.4 %all-to-all-done.1.refs_0_ = bf16[32,136,768]{2,1,0:T(8,128)(2,1)} async-done(((bf16[32,136,768]{2,1,0:T(8,128)(2,1)}), bf16[32,136,768]{2,1,0:T(8,128)(2,1)}, u32[]{:S(2)}, u32[]{:S(2)}) %all-to-all-start.1) | async-done | bytes 6684704 | tf_op jit(solution)/shard_map/all_to_all | solution.py:261
  123.9 0.9 fusion.4
  125.7 10.8 %shard_map.61 = (bf16[8,264,768]{2,1,0:T(8,128)(2,1)}, f32[8,512,256]{2,1,0:T(8,128)}) custom-call(s32[1]{0:T(128)} %bitcast.2.me_ref, bf16[32,136,768]{2,1,0:T(8,128)(2,1)} %all-to-all-done.1.refs_0_, bf16[8,256,1024]{2,1,0:T(8,128)(2,1)} %bitcast.23, s32[8,1,512]{2,1,0:T(1,128)} %reshape.60.refs_2_), custom_call_target="tpu_custom_call" | custom-call | flops 3221225472 | bytes 20971520 | tf_op jit(solution)/shard_map/pallas_call | solution.py:211
  136.5 7.9 %shard_map.60 = bf16[32,128,256]{2,1,0:T(8,128)(2,1)} custom-call(s32[1,2048]{1,0:T(1,128)} %get-tuple-element.15.slot_ref, bf16[2048,1024]{1,0:T(8,128)(2,1)} %points_ref.3), custom_call_target="tpu_custom_call" | custom-call | flops 4294967296 | bytes 3145728 | tf_op jit(solution)/shard_map/pallas_call | solution.py:118
  144.4 34.9 %all_to_all.28.refs_0_ = bf16[32,128,256]{2,1,0:T(8,128)(2,1)} all-to-all(bf16[32,128,256]{2,1,0:T(8,128)(2,1)} %shard_map.60), channel_id=1, replica_groups=mesh['x'=4,'c'=2,'z'=8,'y'=4] {'x','c','y'}, dimensions={0} | all-to-all | bytes 4194304 | tf_op jit(solution)/shard_map/all_to_all | solution.py:261
  179.3 8.5 %shard_map.62 = (bf16[256,256]{1,0:T(8,128)(2,1)}, bf16[256,256]{1,0:T(8,128)(2,1)}, bf16[256,256]{1,0:T(8,128)(2,1)}, bf16[256,256]{1,0:T(8,128)(2,1)}, bf16[25...) custom-call(s32[1]{0:T(128)} %bitcast.2.me_ref, ...), custom_call_target="tpu_custom_call" | custom-call | flops 1073741824 | bytes 12582912 | tf_op jit(solution)/shard_map/pallas_call | solution.py:211
  187.9 4.9 %all-to-all-start.2 = ((bf16[32,128,256]{2,1,0:T(8,128)(2,1)}), bf16[32,128,256]{2,1,0:T(8,128)(2,1)S(1)}, u32[]{:S(2)}, u32[]{:S(2)}) async-start(bf16[32,128,256]{2,1,0:T(8,128)(2,1)} %get-tuple-element.18), calls=%async_computation.2 | async-start | bytes 4194304 | tf_op jit(solution)/shard_map/all_to_all | solution.py:261
  192.8 7.0 %collective-permute-start = (bf16[256,256]{1,0:T(8,128)(2,1)S(1)}, bf16[256,256]{1,0:T(8,128)(2,1)S(1)}, u32[]{:S(2)}, u32[]{:S(2)}) collective-permute-start(bf16[256,256]{1,0:T(8,128)(2,1)S(1)} %copy-done.8), channel_id=1, source_target_pairs={{0,16},{4,20},{8,24},{12,28},{16,0},{20,4},{24,8},{28,12},{1,17},{... | collective-permute-start | bytes 393224 | tf_op jit(solution)/shard_map/ppermute | solution.py:267
  199.8 3.3 %collective-permute-start.2 = (bf16[256,256]{1,0:T(8,128)(2,1)S(1)}, bf16[256,256]{1,0:T(8,128)(2,1)S(1)}, u32[]{:S(2)}, u32[]{:S(2)}) collective-permute-start(bf16[256,256]{1,0:T(8,128)(2,1)S(1)} %copy-done.6), channel_id=1, source_target_pairs={{0,12},{4,16},{8,20},{12,24},{16,28},{20,0},{24,4},{28,8},{1,13},{... | collective-permute-start | bytes 393224 | tf_op jit(solution)/shard_map/ppermute | solution.py:267
  203.1 0.9 collective-permute-start.3
  204.0 1.6 collective-permute-start.4
  205.6 6.0 %collective-permute-start.5 = (bf16[256,256]{1,0:T(8,128)(2,1)S(1)}, bf16[256,256]{1,0:T(8,128)(2,1)S(1)}, u32[]{:S(2)}, u32[]{:S(2)}) collective-permute-start(bf16[256,256]{1,0:T(8,128)(2,1)S(1)} %copy-done.3), channel_id=1, source_target_pairs={{0,28},{4,0},{8,4},{12,8},{16,12},{20,16},{24,20},{28,24},{1,29},{... | collective-permute-start | bytes 393224 | tf_op jit(solution)/shard_map/ppermute | solution.py:267
  211.6 3.9 %collective-permute-done.1 = bf16[256,256]{1,0:T(8,128)(2,1)S(1)} collective-permute-done((bf16[256,256]{1,0:T(8,128)(2,1)S(1)}, bf16[256,256]{1,0:T(8,128)(2,1)S(1)}, u32[]{:S(2)}, u32[]{:S(2)}) %collective-permute-start.1) | collective-permute-done | bytes 131104 | tf_op jit(solution)/shard_map/ppermute | solution.py:267
  215.5 3.8 %collective-permute-done.2 = bf16[256,256]{1,0:T(8,128)(2,1)S(1)} collective-permute-done((bf16[256,256]{1,0:T(8,128)(2,1)S(1)}, bf16[256,256]{1,0:T(8,128)(2,1)S(1)}, u32[]{:S(2)}, u32[]{:S(2)}) %collective-permute-start.2) | collective-permute-done | bytes 131104 | tf_op jit(solution)/shard_map/ppermute | solution.py:267
  219.2 1.9 collective-permute-done.3
  221.1 2.5 collective-permute-done.5
  224.5 1.0 fusion.3
  225.6 2.0 copy_bitcast_fusion
  227.6 5.7 %all-to-all-start.3 = ((bf16[256,8,128]{2,0,1:T(8,128)(2,1)}), bf16[256,8,128]{2,0,1:T(8,128)(2,1)S(1)}, u32[]{:S(2)}, u32[]{:S(2)}) async-start(bf16[256,8,128]{2,0,1:T(8,128)(2,1)} %copy_bitcast_fusion), calls=%async_computation.4 | async-start | bytes 1048576 | tf_op jit(solution)/shard_map/all_to_all | solution.py:299
  233.3 9.6 %shard_map.63 = bf16[2048,256]{1,0:T(8,128)(2,1)} custom-call(s32[1,2048]{1,0:T(1,128)} %get-tuple-element.15.slot_ref, bf16[4096,256]{1,0:T(8,128)(2,1)} %bitcast.25), custom_call_target="tpu_custom_call" | custom-call | flops 4294967296 | bytes 3145728 | tf_op jit(solution)/shard_map/pallas_call | solution.py:243
  243.0 1.0 convert_element_type.86
  (36 shorter events, 2.0 us)
Async XLA Ops:
  7.2 118.5 %all-gather.3.cloned.1.call-start = ((), (), s32[]{:S(2)}) async-start(), calls=%async_computation.6 | async-start | bytes 4718592 | tf_op jit(solution)/shard_map/all_gather | solution.py:277
  31.8 92.1 %all-to-all-start.1 = ((bf16[32,136,768]{2,1,0:T(8,128)(2,1)}), bf16[32,136,768]{2,1,0:T(8,128)(2,1)}, u32[]{:S(2)}, u32[]{:S(2)}) async-start(bf16[32,136,768]{2,1,0:T(8,128)(2,1)} %get-tuple-element.16), calls=%async_computation.1 | async-start | bytes 13369344 | tf_op jit(solution)/shard_map/all_to_all | solution.py:261
  40.4 183.4 %reduce-scatter.2.cloned.1.call-start = ((), (), s32[]{:S(2)}) async-start(), calls=%async_computation.5 | async-start | bytes 3649536 | tf_op jit(solution)/shard_map/reduce_scatter | solution.py:290
  187.8 4.9 %copy-start.8 = (bf16[256,256]{1,0:T(8,128)(2,1)S(1)}, bf16[256,256]{1,0:T(8,128)(2,1)}, u32[]{:S(2)}) copy-start(bf16[256,256]{1,0:T(8,128)(2,1)} %get-tuple-element.21) | copy-start | bytes 393220
  187.8 11.9 %copy-start.7 = (bf16[256,256]{1,0:T(8,128)(2,1)S(1)}, bf16[256,256]{1,0:T(8,128)(2,1)}, u32[]{:S(2)}) copy-start(bf16[256,256]{1,0:T(8,128)(2,1)} %get-tuple-element.22) | copy-start | bytes 393220
  187.9 11.9 %copy-start.6 = (bf16[256,256]{1,0:T(8,128)(2,1)S(1)}, bf16[256,256]{1,0:T(8,128)(2,1)}, u32[]{:S(2)}) copy-start(bf16[256,256]{1,0:T(8,128)(2,1)} %get-tuple-element.23) | copy-start | bytes 393220
  187.9 15.2 %copy-start.5 = (bf16[256,256]{1,0:T(8,128)(2,1)S(1)}, bf16[256,256]{1,0:T(8,128)(2,1)}, u32[]{:S(2)}) copy-start(bf16[256,256]{1,0:T(8,128)(2,1)} %get-tuple-element.24) | copy-start | bytes 393220
  187.9 16.1 %copy-start.4 = (bf16[256,256]{1,0:T(8,128)(2,1)S(1)}, bf16[256,256]{1,0:T(8,128)(2,1)}, u32[]{:S(2)}) copy-start(bf16[256,256]{1,0:T(8,128)(2,1)} %get-tuple-element.25) | copy-start | bytes 393220
  187.9 17.7 %copy-start.3 = (bf16[256,256]{1,0:T(8,128)(2,1)S(1)}, bf16[256,256]{1,0:T(8,128)(2,1)}, u32[]{:S(2)}) copy-start(bf16[256,256]{1,0:T(8,128)(2,1)} %get-tuple-element.26) | copy-start | bytes 393220
  187.9 27.6 %copy-start.2 = (bf16[256,256]{1,0:T(8,128)(2,1)S(1)}, bf16[256,256]{1,0:T(8,128)(2,1)}, u32[]{:S(2)}) copy-start(bf16[256,256]{1,0:T(8,128)(2,1)} %get-tuple-element.27) | copy-start | bytes 393220
  187.9 35.7 %copy-start.1 = (bf16[256,256]{1,0:T(8,128)(2,1)S(1)}, bf16[256,256]{1,0:T(8,128)(2,1)}, u32[]{:S(2)}) copy-start(bf16[256,256]{1,0:T(8,128)(2,1)} %get-tuple-element.20) | copy-start | bytes 393220
  187.9 39.7 %all-to-all-start.2 = ((bf16[32,128,256]{2,1,0:T(8,128)(2,1)}), bf16[32,128,256]{2,1,0:T(8,128)(2,1)S(1)}, u32[]{:S(2)}, u32[]{:S(2)}) async-start(bf16[32,128,256]{2,1,0:T(8,128)(2,1)} %get-tuple-element.18), calls=%async_computation.2 | async-start | bytes 4194304 | tf_op jit(solution)/shard_map/all_to_all | solution.py:261
  192.8 12.8 %collective-permute-start = (bf16[256,256]{1,0:T(8,128)(2,1)S(1)}, bf16[256,256]{1,0:T(8,128)(2,1)S(1)}, u32[]{:S(2)}, u32[]{:S(2)}) collective-permute-start(bf16[256,256]{1,0:T(8,128)(2,1)S(1)} %copy-done.8), channel_id=1, source_target_pairs={{0,16},{4,20},{8,24},{12,28},{16,0},{20,4},{24,8},{28,12},{1,17},{... | collective-permute-start | bytes 393224 | tf_op jit(solution)/shard_map/ppermute | solution.py:267
  199.8 15.7 %collective-permute-start.1 = (bf16[256,256]{1,0:T(8,128)(2,1)S(1)}, bf16[256,256]{1,0:T(8,128)(2,1)S(1)}, u32[]{:S(2)}, u32[]{:S(2)}) collective-permute-start(bf16[256,256]{1,0:T(8,128)(2,1)S(1)} %copy-done.7), channel_id=1, source_target_pairs={{0,20},{4,24},{8,28},{12,0},{16,4},{20,8},{24,12},{28,16},{1,21},{... | collective-permute-start | bytes 393224 | tf_op jit(solution)/shard_map/ppermute | solution.py:267
  199.8 19.4 %collective-permute-start.2 = (bf16[256,256]{1,0:T(8,128)(2,1)S(1)}, bf16[256,256]{1,0:T(8,128)(2,1)S(1)}, u32[]{:S(2)}, u32[]{:S(2)}) collective-permute-start(bf16[256,256]{1,0:T(8,128)(2,1)S(1)} %copy-done.6), channel_id=1, source_target_pairs={{0,12},{4,16},{8,20},{12,24},{16,28},{20,0},{24,4},{28,8},{1,13},{... | collective-permute-start | bytes 393224 | tf_op jit(solution)/shard_map/ppermute | solution.py:267
  203.1 18.1 %collective-permute-start.3 = (bf16[256,256]{1,0:T(8,128)(2,1)S(1)}, bf16[256,256]{1,0:T(8,128)(2,1)S(1)}, u32[]{:S(2)}, u32[]{:S(2)}) collective-permute-start(bf16[256,256]{1,0:T(8,128)(2,1)S(1)} %copy-done.5), channel_id=1, source_target_pairs={{0,24},{4,28},{8,0},{12,4},{16,8},{20,12},{24,16},{28,20},{1,25},{... | collective-permute-start | bytes 393224 | tf_op jit(solution)/shard_map/ppermute | solution.py:267
  204.0 17.1 %collective-permute-start.4 = (bf16[256,256]{1,0:T(8,128)(2,1)S(1)}, bf16[256,256]{1,0:T(8,128)(2,1)S(1)}, u32[]{:S(2)}, u32[]{:S(2)}) collective-permute-start(bf16[256,256]{1,0:T(8,128)(2,1)S(1)} %copy-done.4), channel_id=1, source_target_pairs={{0,8},{4,12},{8,16},{12,20},{16,24},{20,28},{24,0},{28,4},{1,9},{5... | collective-permute-start | bytes 393224 | tf_op jit(solution)/shard_map/ppermute | solution.py:267
  205.6 18.0 %collective-permute-start.5 = (bf16[256,256]{1,0:T(8,128)(2,1)S(1)}, bf16[256,256]{1,0:T(8,128)(2,1)S(1)}, u32[]{:S(2)}, u32[]{:S(2)}) collective-permute-start(bf16[256,256]{1,0:T(8,128)(2,1)S(1)} %copy-done.3), channel_id=1, source_target_pairs={{0,28},{4,0},{8,4},{12,8},{16,12},{20,16},{24,20},{28,24},{1,29},{... | collective-permute-start | bytes 393224 | tf_op jit(solution)/shard_map/ppermute | solution.py:267
  215.5 8.1 %collective-permute-start.6 = (bf16[256,256]{1,0:T(8,128)(2,1)S(1)}, bf16[256,256]{1,0:T(8,128)(2,1)S(1)}, u32[]{:S(2)}, u32[]{:S(2)}) collective-permute-start(bf16[256,256]{1,0:T(8,128)(2,1)S(1)} %copy-done.2), channel_id=1, source_target_pairs={{0,4},{4,8},{8,12},{12,16},{16,20},{20,24},{24,28},{28,0},{1,5},{5... | collective-permute-start | bytes 393224 | tf_op jit(solution)/shard_map/ppermute | solution.py:267
  227.6 5.7 %copy-start = (bf16[32,128,256]{2,1,0:T(8,128)(2,1)}, bf16[32,128,256]{2,1,0:T(8,128)(2,1)S(1)}, u32[]{:S(2)}) copy-start(bf16[32,128,256]{2,1,0:T(8,128)(2,1)S(1)} %all-to-all-done.2) | copy-start | bytes 6291460
  227.6 15.3 %all-to-all-start.3 = ((bf16[256,8,128]{2,0,1:T(8,128)(2,1)}), bf16[256,8,128]{2,0,1:T(8,128)(2,1)S(1)}, u32[]{:S(2)}, u32[]{:S(2)}) async-start(bf16[256,8,128]{2,0,1:T(8,128)(2,1)} %copy_bitcast_fusion), calls=%async_computation.4 | async-start | bytes 1048576 | tf_op jit(solution)/shard_map/all_to_all | solution.py:299
Sparse Core Ops, SparseCore 0:
  10.3 58.3 all-gather.2
  136.7 47.9 reduce-scatter.1
